TPU v7x, 32 devices: a whole 2x2x4 slice. The times are simulated.
32 devices in a mesh: replica: 4 (over y, x), fsdp: 8 (over z, core).
Axes of the slice: x: 2, y: 2, z: 4, core: 2. Of those that a mesh axis runs over, the one named last changes fastest.
Arguments:
- base_weights: float32 [8192, 1024], P('fsdp'), may hold values from -5 to 5, as said below
- inner_weights: bfloat16 [4, 8192, 1024], P('replica', 'fsdp'), may hold values from -12 to 12, as said below
- momentum: float32 [8192, 1024], P(('fsdp', 'replica')), may hold values from -1 to 1
Outputs:
- new_base: float32 [8192, 1024], P('fsdp')
- new_momentum: float32 [8192, 1024], P(('fsdp', 'replica'))
- new_inner: bfloat16 [4, 8192, 1024], P('replica', 'fsdp')
Inputs may be any that keep to these rules, and one draw needn't show every extreme that they name: `base_weights`: the shared outer weights, multiples of 2 ** -16. `inner_weights`: each replica's weights after its inner steps, multiples of 2 ** -16.
All inputs are finite; a program needn't handle non-finite values.
Results may differ from a plain program's by a relative error of at most 0.0015.
Values may be sent and summed in bfloat16 or wider, within the bound.
A program may use at most 64 MiB of HBM per device.

v0:
```python
import jax
import jax.numpy as jnp
from jax import lax
from jax.sharding import PartitionSpec as P

D = 8192
KVW = 1024
BLOCK = 128


code_limit = 448.0
outer_rate = 0.7
outer_momentum = 0.9
blend_share = 0.5
clip_rms = 0.02
epsilon = 1e-06
smallest_normal = 0.015625


def power_two(exponent):
    unit_ones = jnp.ones_like(exponent)
    upward = jnp.left_shift(unit_ones, jnp.maximum(exponent, 0)).astype(jnp.float32)
    downward = jnp.left_shift(unit_ones, jnp.maximum(-exponent, 0)).astype(jnp.float32)
    return upward / downward


def exponent_above(target):
    estimate = jnp.ceil(jnp.log2(target)).astype(jnp.int32)
    estimate = jnp.where(target <= power_two(estimate - 1), estimate - 1, estimate)
    return jnp.where(target > power_two(estimate), estimate + 1, estimate)


def exponent_below(target):
    estimate = jnp.floor(jnp.log2(target)).astype(jnp.int32)
    estimate = jnp.where(target >= power_two(estimate + 1), estimate + 1, estimate)
    return jnp.where(target < power_two(estimate), estimate - 1, estimate)


def encode(deltas):
    shaped = deltas.reshape(deltas.shape[0], deltas.shape[1] // BLOCK, BLOCK)
    block_peaks = jnp.max(jnp.abs(shaped), axis=2)
    scales = power_two(exponent_above((block_peaks + epsilon) / code_limit))
    code_units = shaped / scales[:, :, None]
    magnitude = jnp.abs(code_units)
    quantum = power_two(exponent_below(jnp.maximum(magnitude, smallest_normal)) - 3)
    steps_count = jnp.floor(magnitude / quantum + 0.5)
    code_values = (jnp.where(code_units < 0, -steps_count, steps_count) * quantum).astype(
        jnp.bfloat16
    )
    return (code_values, scales)


def shards(base_weights, inner_weights, momentum):
    replicas = lax.axis_size("replica")
    local_rows, columns_all = base_weights.shape
    owned_rows = local_rows // replicas
    replica_copy = inner_weights[0]
    deltas = base_weights - replica_copy.astype(jnp.float32)
    code_values, scales = encode(deltas)
    decoded = (code_values.astype(jnp.float32) * scales[:, :, None]).reshape(
        local_rows, columns_all
    )
    summed = lax.psum_scatter(
        decoded.astype(jnp.bfloat16), "replica", scatter_dimension=0, tiled=True
    ).astype(jnp.float32)
    outer_grad = summed / replicas
    owner_index = lax.axis_index("replica")
    base_owned = lax.dynamic_slice_in_dim(base_weights, owner_index * owned_rows, owned_rows, 0)
    grad_sq = lax.psum(jnp.sum(outer_grad * outer_grad), ("replica", "fsdp"))
    clip_factor = jnp.minimum(1.0, clip_rms / jnp.sqrt(grad_sq / (D * KVW) + epsilon))
    step_term = clip_factor * outer_grad
    new_momentum = outer_momentum * momentum + step_term
    owned_base = base_owned - outer_rate * (step_term + outer_momentum * new_momentum)
    new_base = lax.all_gather(owned_base, "replica", axis=0, tiled=True)
    blended = blend_share * replica_copy.astype(jnp.float32) + (1.0 - blend_share) * new_base
    new_inner = blended.astype(jnp.bfloat16)
    return (new_base, new_momentum, new_inner[None])


def solution(mesh):
    placed = (P("fsdp", None), P("replica", "fsdp", None), P(("fsdp", "replica"), None))
    return jax.shard_map(
        shards,
        mesh=mesh,
        in_specs=placed,
        out_specs=(P("fsdp", None), P(("fsdp", "replica"), None), P("replica", "fsdp", None)),
        check_vma=False,
    )
```

profile of v0, /device:TPU:0, one launch (start us, length us, event | category | flops | bytes accessed | tf_op | source)
XLA Modules:
  0.0 180.1 jit_solution(5941321848288735031)
XLA Ops:
  7.2 0.0 reduce-scatter.2.cloned.1.call-start
  7.2 3.6 %abs_bitcast_fusion = f32[128,8,8,128]{3,1,2,0:T(8,128)S(1)} fusion(f32[1024,1024]{1,0:T(8,128)} %param.3, bf16[1,1024,1024]{2,1,0:T(8,128)(2,1)} %param.4), kind=kLoop, calls=%fused_computation.27 | loop fusion | flops 3145728 | bytes 10485760
  10.8 3.0 %copy.9 = f32[128,8,8,128]{3,2,1,0:T(8,128)} copy(f32[128,8,8,128]{3,1,2,0:T(8,128)S(1)} %abs_bitcast_fusion) | data formatting | bytes 8388608
  13.8 0.0 copy-start.1
  13.8 3.5 %reduce_max.9 = f32[1024,8]{1,0:T(8,128)S(1)} reduce(f32[1024,8,128]{2,1,0:T(8,128)} %bitcast.21, f32[]{:T(128)} %constant.25.clone.1), dimensions={2}, to_apply=%region_0.0 | reduce | flops 1040384 | bytes 4227076 | tf_op jit(solution)/shard_map/reduce_max | solution.py:41
  17.3 0.2 copy.7
  17.5 0.1 convert_divide_fusion
  17.6 0.2 copy.8
  17.8 0.0 copy-start
  17.8 1.1 div.71
  18.9 0.0 copy-done.1
  18.9 1.0 copy-done
  20.0 0.0 copy-start.3
  20.0 9.8 %fusion.12 = bf16[1024,1024]{1,0:T(8,128)(2,1)} fusion(f32[128,8,8,128]{3,2,1,0:T(8,128)S(1)} %bitcast.20, f32[1024,1024]{1,0:T(8,128)S(1)} %copy-done, bf16[1,1024,1024]{2,1,0:T(8,128)(2,1)S(1)} %copy-done.1), kind=kLoop, calls=%fused_computation.21 | loop fusion | flops 53477376 | bytes 12582912 | tf_op jit(solution)/shard_map/convert_element_type | solution.py:64
  29.8 0.0 reduce-scatter.2.cloned.1.call-update
  29.8 0.0 all-gather.2.cloned.1.call-start
  29.9 38.0 %reduce-scatter.2.cloned.1.call-done = bf16[256,1024]{1,0:T(8,128)(2,1)} async-done(((bf16[1024,1024]{1,0:T(8,128)(2,1)}), bf16[256,1024]{1,0:T(8,128)(2,1)}) %reduce-scatter.2.cloned.1.call-update) | async-done | bytes 524304 | tf_op jit(solution)/shard_map/reduce_scatter | solution.py:63
  67.9 1.9 %fusion.22 = f32[]{:T(128)} fusion(bf16[256,1024]{1,0:T(8,128)(2,1)} %reduce-scatter.2.cloned.1.call-done), kind=kLoop, calls=%fused_computation.36 | loop fusion | flops 1048575 | bytes 524292 | tf_op jit(solution)/shard_map/reduce_sum | solution.py:69
  69.8 39.5 %psum.7 = f32[]{:T(128)} all-reduce(f32[]{:T(128)} %fusion.22), channel_id=1, replica_groups=mesh['replica'=4,'fsdp'=8] {'replica','fsdp'}, use_global_device_ids=true, to_apply=%region_3.4 | all-reduce | flops 1 | bytes 8 | tf_op jit(solution)/shard_map/psum | solution.py:69
  110.0 0.0 copy-done.3
  110.0 3.1 %fusion.20 = (f32[256,1024]{1,0:T(8,128)}, f32[256,1024]{1,0:T(8,128)}) fusion(bf16[256,1024]{1,0:T(8,128)(2,1)} %reduce-scatter.2.cloned.1.call-done, f32[1024,1024]{1,0:T(8,128)} %param.3, s32[]{:T(128)S(6)} %select_n.32, f32[]{:T(128)S(6)} %mul.45, f32[256,1024]{1,0:T(8,128)S(1)} %copy-done.3), kind=kLoop, calls=%fused_computation.34 | loop fusion | flops 2097152 | bytes 4718600 | tf_op jit(solution)/shard_map/sub | solution.py:73
  113.1 0.0 all-gather.2.cloned.1.call-update
  113.1 53.7 %all-gather.2.cloned.1.call-done = f32[1024,1024]{1,0:T(8,128)} async-done(((f32[256,1024]{1,0:T(8,128)}), f32[1024,1024]{1,0:T(8,128)}) %all-gather.2.cloned.1.call-update) | async-done | bytes 4194320 | tf_op jit(solution)/shard_map/all_gather | solution.py:74
  166.8 0.0 copy-start.2
  166.8 4.4 %fusion.16 = bf16[1,1024,1024]{2,1,0:T(8,128)(2,1)} fusion(f32[1024,1024]{1,0:T(8,128)} %all-gather.2.cloned.1.call-done, bf16[1,1024,1024]{2,1,0:T(8,128)(2,1)S(1)} %copy-done.1), kind=kLoop, calls=%fused_computation.28 | loop fusion | flops 4194304 | bytes 8388608 | tf_op jit(solution)/shard_map/broadcast_in_dim | solution.py:77
  171.2 0.0 copy-done.2
  171.2 2.0 %copy.13 = f32[1024,1024]{1,0:T(8,128)} copy(f32[1024,1024]{1,0:T(8,128)S(1)} %copy-done.2) | data formatting | bytes 8388608
Async XLA Ops:
  7.2 60.7 %reduce-scatter.2.cloned.1.call-start = ((), (), s32[]{:S(2)}) async-start(), calls=%async_computation.1 | async-start | bytes 2621440 | tf_op jit(solution)/shard_map/reduce_scatter | solution.py:63
  13.8 5.1 %copy-start.1 = (bf16[1,1024,1024]{2,1,0:T(8,128)(2,1)S(1)}, bf16[1,1024,1024]{2,1,0:T(8,128)(2,1)}, u32[]{:S(2)}) copy-start(bf16[1,1024,1024]{2,1,0:T(8,128)(2,1)} %param.4) | copy-start | bytes 6291460
  17.8 2.2 %copy-start = (f32[1024,1024]{1,0:T(8,128)S(1)}, f32[1024,1024]{1,0:T(8,128)}, u32[]{:S(2)}) copy-start(f32[1024,1024]{1,0:T(8,128)} %param.3) | copy-start | bytes 12582916
  20.0 90.0 %copy-start.3 = (f32[256,1024]{1,0:T(8,128)S(1)}, f32[256,1024]{1,0:T(8,128)}, u32[]{:S(2)}) copy-start(f32[256,1024]{1,0:T(8,128)} %param.5) | copy-start | bytes 3145732
  29.8 137.0 %all-gather.2.cloned.1.call-start = ((), (), s32[]{:S(2)}) async-start(), calls=%async_computation.2 | async-start | bytes 5242880 | tf_op jit(solution)/shard_map/all_gather | solution.py:74
  166.8 4.4 %copy-start.2 = (f32[1024,1024]{1,0:T(8,128)S(1)}, f32[1024,1024]{1,0:T(8,128)}, u32[]{:S(2)}) copy-start(f32[1024,1024]{1,0:T(8,128)} %all-gather.2.cloned.1.call-done) | copy-start | bytes 12582916
Sparse Core Ops, SparseCore 0:
  29.9 37.9 reduce-scatter.1
  113.2 53.5 all-gather.1
where the time goes:
time: 180 us
  waiting for transfers between devices  91.8 us (51%)
  blocking collectives  39.5 us (22%)
  other arithmetic  26.4 us (15%)
  between operations  14.8 us (8%)
  local copies, waits for them, and re-layouts  7.57 us (4%)
    all_gather x1, waiting for transfers between devices, shards(): new_base = lax.all_gather(owned_base, 'replica', axis=0, tiled=True)  53.7 us
    psum x1, blocking collectives, shards(): grad_sq = lax.psum(jnp.sum(outer_grad * outer_grad), ('replica', 'fsdp'))  39.5 us
    reduce_scatter x1, waiting for transfers between devices, shards(): lax.psum_scatter(decoded.astype(jnp.bfloat16), 'replica', scatter_dimensi...  38 us
    convert_element_type x1, other arithmetic, shards(): decoded.astype(jnp.bfloat16)  9.81 us
    unnamed x10, local copies, waits for them, and re-layouts  6.08 us
    broadcast_in_dim x1, other arithmetic, shards(): return (new_base, new_momentum, new_inner[None])  4.44 us
  transfers between devices with their start and end apart: 2, of which 2 were waited for; matrix products, arithmetic and copies ran while one was open for 0% of the time, Pallas kernels for 0%

commit v1 on v0

v1 whole, which is shorter than its diff:
```python
import functools

import jax
import jax.numpy as jnp
from jax import lax
from jax.experimental import pallas as pl
from jax.experimental.pallas import tpu as pltpu
from jax.sharding import PartitionSpec as P

BLOCK = 128
HALF_GROUPS = 2

code_limit = 448.0
outer_rate = 0.7
outer_momentum = 0.9
blend_share = 0.5
clip_rms = 0.02
epsilon = 1e-06

MESH = pl.DeviceIdType.MESH


def decoded_deltas(deltas):
    peaks = jnp.max(jnp.abs(deltas), axis=1, keepdims=True) + epsilon
    rough = peaks * (1.0 / code_limit)
    wide = rough * (2.0**23 + 1.0)
    power = wide - (wide - rough)
    scales = jnp.where(power * code_limit < peaks, power + power, power)
    nudged = deltas * (1.0 + 2.0**-23)
    wide_deltas = nudged * (2.0**20 + 1.0)
    four_bits = wide_deltas - (wide_deltas - nudged)
    shift = scales * (1.5 * 2.0**14)
    fixed_step = (nudged + shift) - shift
    return jnp.where(jnp.abs(deltas) < scales * 2.0**-6, fixed_step, four_bits)


def grid_sides(replicas):
    side = 1 << (replicas.bit_length() // 2)
    while replicas % side:
        side -= 1
    return side, replicas // side


def kernel(
    dims,
    base_hbm, inner_hbm, momentum_hbm,
    new_base, new_momentum, new_inner,
    base_v, inner_v, momentum_v, dec, first, second, grad, update,
    square_mine, square_near, square_row, square_far,
    load_sems, send_one, recv_one, send_two, recv_two, send_all, recv_all,
    near_send, near_recv, far_send, far_recv,
):
    replicas, shards_count, rows, columns, groups, total = dims
    width = columns // groups
    span_x, span_y = grid_sides(replicas)
    tile = min(32, rows)
    me = lax.axis_index("replica")
    row_me = lax.axis_index("fsdp")
    me_x, me_y = lax.rem(me, span_x), me // span_x

    def spans(g):
        return (span_x, span_y) if g % 2 == 0 else (span_y, span_x)

    def owner(g, dp, dq):
        dx, dy = (dp, dq) if g % 2 == 0 else (dq, dp)
        return lax.rem(me_y + dy, span_y) * span_x + lax.rem(me_x + dx, span_x)

    def near(step):
        return lax.rem(me + step, replicas)

    def far(step):
        return lax.rem(row_me + step, shards_count)

    def row_start(index):
        return pl.multiple_of(index * rows, rows)

    load_order = [(dx, dy) for dy in reversed(range(span_y)) for dx in reversed(range(span_x))]
    loads = []
    for at, (dx, dy) in enumerate(load_order):
        here = pl.ds(row_start(owner(0, dx, dy)), rows)
        pair = (
            pltpu.make_async_copy(base_hbm.at[here], base_v.at[here], load_sems.at[at, 0]),
            pltpu.make_async_copy(inner_hbm.at[0, here], inner_v.at[here], load_sems.at[at, 1]),
        )
        for copy in pair:
            copy.start()
        loads.append(pair)
    momentum_load = pltpu.make_async_copy(momentum_hbm, momentum_v, load_sems.at[replicas, 0])
    momentum_load.start()

    barrier = pltpu.get_barrier_semaphore()
    for step in range(1, replicas):
        pl.semaphore_signal(barrier, inc=1, device_id={"replica": near(step)}, device_id_type=MESH)
    for step in range(1, shards_count):
        pl.semaphore_signal(barrier, inc=1, device_id={"fsdp": far(step)}, device_id_type=MESH)

    def encode(g, dp, dq):
        slot = dp * spans(g)[1] + dq
        start = row_start(owner(g, dp, dq))

        @pl.loop(0, rows // tile)
        def _(t):
            at = pl.ds(pl.multiple_of(start + t * tile, tile), tile)
            to = pl.ds(pl.multiple_of(t * tile, tile), tile)
            for c in range(0, width, BLOCK):
                cols = pl.ds(g * width + c, BLOCK)
                deltas = base_v[at, cols] - inner_v[at, cols].astype(jnp.float32)
                dec[g, slot, to, pl.ds(c, BLOCK)] = decoded_deltas(deltas).astype(jnp.bfloat16)

    def copy_one(g, dp, dq):
        slot = dp * spans(g)[1] + dq
        return pltpu.make_async_remote_copy(
            src_ref=dec.at[g, slot], dst_ref=first.at[g, slot],
            send_sem=send_one.at[g, slot], recv_sem=recv_one.at[g, slot],
            device_id={"replica": owner(g, dp, 0)}, device_id_type=MESH,
        )

    def copy_two(g, dq):
        return pltpu.make_async_remote_copy(
            src_ref=dec.at[g, dq], dst_ref=second.at[g, dq],
            send_sem=send_two.at[g, dq], recv_sem=recv_two.at[g, dq],
            device_id={"replica": owner(g, 0, dq)}, device_id_type=MESH,
        )

    def copy_all(g, dp, dq, source):
        np, nq = spans(g)
        slot = ((np - dp) % np) * nq + (source if dp else (nq - dq) % nq)
        return pltpu.make_async_remote_copy(
            src_ref=update.at[g, source if dp else 0], dst_ref=update.at[g, slot],
            send_sem=send_all.at[g, slot], recv_sem=recv_all.at[g, slot],
            device_id={"replica": owner(g, dp, dq)}, device_id_type=MESH,
        )

    waited = set()

    def await_load(g, dp, dq):
        key = (dp, dq) if g % 2 == 0 else (dq, dp)
        if key not in waited:
            waited.add(key)
            for copy in loads[load_order.index(key)]:
                copy.wait()

    sends = []
    greeted = False
    most = max(span_x, span_y)
    for dq in reversed(range(most)):
        for dp in reversed(range(1, most)):
            for g in range(groups):
                np, nq = spans(g)
                if dp < np and dq < nq:
                    await_load(g, dp, dq)
                    encode(g, dp, dq)
                    if not greeted:
                        pl.semaphore_wait(barrier, replicas - 1 + shards_count - 1)
                        greeted = True
                    copy = copy_one(g, dp, dq)
                    copy.start()
                    sends.append(copy)
    for dq in reversed(range(most)):
        for g in range(groups):
            if dq < spans(g)[1]:
                await_load(g, 0, dq)
                encode(g, 0, dq)

    for dq in reversed(range(most)):
        for g in range(groups):
            np, nq = spans(g)
            if dq >= nq:
                continue
            for dp in range(1, np):
                copy_one(g, dp, dq).wait_recv()

            @pl.loop(0, rows // tile)
            def _(t):
                at = pl.ds(pl.multiple_of(t * tile, tile), tile)
                summed = dec[g, dq, at].astype(jnp.float32)
                for dp in range(1, np):
                    summed += first[g, dp * nq + dq, at].astype(jnp.float32)
                if dq:
                    dec[g, dq, at] = summed.astype(jnp.bfloat16)
                else:
                    grad[at, pl.ds(g * width, width)] = summed

            if dq:
                copy = copy_two(g, dq)
                copy.start()
                sends.append(copy)

    squares = jnp.zeros((8, BLOCK), jnp.float32)
    for g in range(groups):
        nq = spans(g)[1]
        for dq in range(1, nq):
            copy_two(g, dq).wait_recv()

        def add(t, squares):
            at = pl.ds(pl.multiple_of(t * tile, tile), tile)
            for c in range(0, width, BLOCK):
                cols = pl.ds(g * width + c, BLOCK)
                summed = grad[at, cols]
                for dq in range(1, nq):
                    summed += second[g, dq, at, pl.ds(c, BLOCK)].astype(jnp.float32)
                outer = summed * (1.0 / replicas)
                grad[at, cols] = outer
                square = outer * outer
                for s in range(0, tile, 8):
                    squares += square[s : s + 8]
            return squares

        squares = lax.fori_loop(0, rows // tile, add, squares)

    square_mine[...] = squares
    near_copies = []
    for step in range(1, replicas):
        copy = pltpu.make_async_remote_copy(
            src_ref=square_mine, dst_ref=square_near.at[step],
            send_sem=near_send.at[step], recv_sem=near_recv.at[step],
            device_id={"replica": near(step)}, device_id_type=MESH,
        )
        copy.start()
        near_copies.append(copy)
    sends += near_copies
    for copy in near_copies:
        copy.wait_recv()
    for step in range(1, replicas):
        squares += square_near[step]
    square_row[...] = squares
    far_copies = []
    for step in range(1, shards_count):
        copy = pltpu.make_async_remote_copy(
            src_ref=square_row, dst_ref=square_far.at[step],
            send_sem=far_send.at[step], recv_sem=far_recv.at[step],
            device_id={"fsdp": far(step)}, device_id_type=MESH,
        )
        copy.start()
        far_copies.append(copy)
    sends += far_copies
    momentum_load.wait()
    for copy in far_copies:
        copy.wait_recv()
    for step in range(1, shards_count):
        squares += square_far[step]
    mean_square = jnp.full((1, BLOCK), jnp.sum(squares), jnp.float32) / total
    clip_factor = jnp.minimum(1.0, clip_rms / jnp.sqrt(mean_square + epsilon))

    for g in range(groups):
        np, nq = spans(g)

        @pl.loop(0, rows // tile)
        def _(t):
            at = pl.ds(pl.multiple_of(t * tile, tile), tile)
            for c in range(0, width, BLOCK):
                cols = pl.ds(g * width + c, BLOCK)
                step_term = clip_factor * grad[at, cols]
                moved = outer_momentum * momentum_v[at, cols] + step_term
                new_momentum[at, cols] = moved
                update[g, 0, at, pl.ds(c, BLOCK)] = (step_term + outer_momentum * moved).astype(
                    jnp.bfloat16
                )

        for dq in range(1, nq):
            copy = copy_all(g, 0, dq, 0)
            copy.start()
            sends.append(copy)
    for g in range(groups):
        for dp in range(1, spans(g)[0]):
            copy = copy_all(g, dp, 0, 0)
            copy.start()
            sends.append(copy)

    def finish(g, dp, dq):
        slot = dp * spans(g)[1] + dq
        start = row_start(owner(g, dp, dq))

        @pl.loop(0, rows // tile)
        def _(t):
            at = pl.ds(pl.multiple_of(start + t * tile, tile), tile)
            to = pl.ds(pl.multiple_of(t * tile, tile), tile)
            cols = pl.ds(g * width, width)
            fresh = base_v[at, cols] - outer_rate * update[g, slot, to].astype(jnp.float32)
            new_base[at, cols] = fresh
            blended = blend_share * inner_v[at, cols].astype(jnp.float32) + (
                1.0 - blend_share
            ) * fresh
            new_inner[0, at, cols] = blended.astype(jnp.bfloat16)

    for g in range(groups):
        finish(g, 0, 0)
    for g in range(groups):
        np, nq = spans(g)
        for dq in range(1, nq):
            copy_all(g, 0, (nq - dq) % nq, 0).wait_recv()
            for dp in range(1, np):
                copy = copy_all(g, dp, 0, dq)
                copy.start()
                sends.append(copy)
            finish(g, 0, dq)
    for dq in range(most):
        for g in range(groups):
            np, nq = spans(g)
            if dq < nq:
                for dp in range(1, np):
                    copy_all(g, (np - dp) % np, 0, dq).wait_recv()
                    finish(g, dp, dq)
    for copy in sends:
        copy.wait_send()


def shards(base_weights, inner_weights, momentum):
    replicas = lax.axis_size("replica")
    shards_count = lax.axis_size("fsdp")
    local_rows, columns = base_weights.shape
    rows = local_rows // replicas
    groups = 2 * HALF_GROUPS
    width = columns // groups
    total = float(local_rows * shards_count * columns)
    dims = (replicas, shards_count, rows, columns, groups, total)
    most = max(grid_sides(replicas))
    dma = pltpu.SemaphoreType.DMA
    blocks = (groups, replicas, rows, width)
    anywhere = pl.BlockSpec(memory_space=pl.ANY)
    vmem = pl.BlockSpec(memory_space=pltpu.VMEM)
    return pl.pallas_call(
        functools.partial(kernel, dims),
        out_shape=(
            jax.ShapeDtypeStruct(base_weights.shape, jnp.float32),
            jax.ShapeDtypeStruct(momentum.shape, jnp.float32),
            jax.ShapeDtypeStruct(inner_weights.shape, jnp.bfloat16),
        ),
        in_specs=[anywhere] * 3,
        out_specs=(vmem, vmem, vmem),
        scratch_shapes=[
            pltpu.VMEM((local_rows, columns), jnp.float32),
            pltpu.VMEM((local_rows, columns), jnp.bfloat16),
            pltpu.VMEM((rows, columns), jnp.float32),
            pltpu.VMEM(blocks, jnp.bfloat16),
            pltpu.VMEM(blocks, jnp.bfloat16),
            pltpu.VMEM((groups, most, rows, width), jnp.bfloat16),
            pltpu.VMEM((rows, columns), jnp.float32),
            pltpu.VMEM(blocks, jnp.bfloat16),
            pltpu.VMEM((8, BLOCK), jnp.float32),
            pltpu.VMEM((replicas, 8, BLOCK), jnp.float32),
            pltpu.VMEM((8, BLOCK), jnp.float32),
            pltpu.VMEM((shards_count, 8, BLOCK), jnp.float32),
            dma((replicas + 1, 2)),
            dma((groups, replicas)),
            dma((groups, replicas)),
            dma((groups, most)),
            dma((groups, most)),
            dma((groups, replicas)),
            dma((groups, replicas)),
            dma((replicas,)),
            dma((replicas,)),
            dma((shards_count,)),
            dma((shards_count,)),
        ],
        compiler_params=pltpu.CompilerParams(collective_id=0, has_side_effects=True),
    )(base_weights, inner_weights, momentum)


def solution(mesh):
    placed = (P("fsdp", None), P("replica", "fsdp", None), P(("fsdp", "replica"), None))
    return jax.shard_map(
        shards,
        mesh=mesh,
        in_specs=placed,
        out_specs=(P("fsdp", None), P(("fsdp", "replica"), None), P("replica", "fsdp", None)),
        check_vma=False,
    )
```

time: 180 us -> 64.6 us (0.36)
  waiting for transfers between devices: 91.8 us -> 0 us
  Pallas kernels: 0 us -> 56.6 us
  blocking collectives: 39.5 us -> 0 us
  other arithmetic: 26.4 us -> 0 us
  between operations: 14.8 us -> 0.66 us
    pallas_call x0 -> x1, Pallas kernels: none -> 56.6 us  [shards(): pl.pallas_call(functools.partial(kernel, dims), out_shape=(jax.ShapeDtype...]
    all_gather x1 -> x0, waiting for transfers between devices: 53.7 us -> none  [shards(): new_base = lax.all_gather(owned_base, 'replica', axis=0, tiled=True)]
    psum x1 -> x0, blocking collectives: 39.5 us -> none  [shards(): grad_sq = lax.psum(jnp.sum(outer_grad * outer_grad), ('replica', 'fsdp'))]
    reduce_scatter x1 -> x0, waiting for transfers between devices: 38 us -> none  [shards(): lax.psum_scatter(decoded.astype(jnp.bfloat16), 'replica', scatter_dimensi...]
    convert_element_type x1 -> x0, other arithmetic: 9.81 us -> none  [shards(): decoded.astype(jnp.bfloat16)]
    broadcast_in_dim x1 -> x0, other arithmetic: 4.44 us -> none  [shards(): return (new_base, new_momentum, new_inner[None])]
    unnamed x1 -> x0, other arithmetic: 3.57 us -> none
    reduce_max x1 -> x0, other arithmetic: 3.51 us -> none  [encode(): block_peaks = jnp.max(jnp.abs(shaped), axis=2)]
  transfers between devices with their start and end apart: 2 -> 0, of which waited for: 2 -> 0; matrix products, arithmetic and copies ran while one was open for 0% -> 0% of each run, Pallas kernels for 0% -> 0%
where the time goes in v1:
time: 64.6 us; the launch traced here: 64.5 us
  Pallas kernels  56.6 us (88%)
  local copies, waits for them, and re-layouts  7.24 us (11%)
  between operations  0.66 us (1%)
    pallas_call x1, Pallas kernels, shards(): pl.pallas_call(functools.partial(kernel, dims), out_shape=(jax.ShapeDtype...  56.6 us
    unnamed x7, local copies, waits for them, and re-layouts  7.24 us

profile of v1, /device:TPU:0, one launch (start us, length us, event | category | flops | bytes accessed | tf_op | source)
XLA Modules:
  0.0 64.5 jit_solution(16654612660270254715)
XLA Ops:
  0.6 56.6 %shard_map.58 = (f32[1024,1024]{1,0:T(8,128)}, f32[256,1024]{1,0:T(8,128)}, bf16[1,1024,1024]{2,1,0:T(8,128)(2,1)}) custom-call(f32[1024,1024]{1,0:T(8,128)} %base_hbm.1, bf16[1,1024,1024]{2,1,0:T(8,128)(2,1)} %inner_hbm.1, f32[256,1024]{1,0:T(8,128)} %momentum_hbm.1), custom_call_target="tpu_custom_call" | custom-call | tf_op jit(solution)/shard_map/pallas_call | solution.py:322
  57.2 0.0 copy-start.1
  57.2 0.0 copy-start
  57.2 4.9 %copy.9 = f32[1024,1024]{1,0:T(8,128)} copy(f32[1024,1024]{1,0:T(8,128)} %get-tuple-element.6) | data formatting | bytes 8388608
  62.2 0.0 copy-done.1
  62.2 1.0 %copy.10 = f32[256,1024]{1,0:T(8,128)} copy(f32[256,1024]{1,0:T(8,128)S(1)} %copy-done.1) | data formatting | bytes 2097152
  63.1 0.0 copy-done
  63.1 1.3 %copy.11 = bf16[1,1024,1024]{2,1,0:T(8,128)(2,1)} copy(bf16[1,1024,1024]{2,1,0:T(8,128)(2,1)S(1)} %copy-done) | data formatting | bytes 4194304
Async XLA Ops:
  57.2 5.0 %copy-start.1 = (f32[256,1024]{1,0:T(8,128)S(1)}, f32[256,1024]{1,0:T(8,128)}, u32[]{:S(2)}) copy-start(f32[256,1024]{1,0:T(8,128)} %get-tuple-element.7) | copy-start | bytes 3145732
  57.2 5.9 %copy-start = (bf16[1,1024,1024]{2,1,0:T(8,128)(2,1)S(1)}, bf16[1,1024,1024]{2,1,0:T(8,128)(2,1)}, u32[]{:S(2)}) copy-start(bf16[1,1024,1024]{2,1,0:T(8,128)(2,1)} %get-tuple-element.8) | copy-start | bytes 6291460

commit v2 on v1

--- a/solution.py
+++ b/solution.py
@@ -305,6 +305,18 @@
         copy.wait_send()
 
 
+def write_out(*refs):
+    sems = refs[-1]
+    parts = len(refs) // 2
+    copies = [
+        pltpu.make_async_copy(refs[i], refs[parts + i], sems.at[i]) for i in range(parts)
+    ]
+    for copy in copies:
+        copy.start()
+    for copy in copies:
+        copy.wait()
+
+
 def shards(base_weights, inner_weights, momentum):
     replicas = lax.axis_size("replica")
     shards_count = lax.axis_size("fsdp")
@@ -317,16 +329,18 @@
     most = max(grid_sides(replicas))
     dma = pltpu.SemaphoreType.DMA
     blocks = (groups, replicas, rows, width)
-    anywhere = pl.BlockSpec(memory_space=pl.ANY)
+    outside = pl.BlockSpec(memory_space=pltpu.HBM)
     vmem = pl.BlockSpec(memory_space=pltpu.VMEM)
-    return pl.pallas_call(
+    in_hbm = functools.partial(pltpu.with_memory_space_constraint, memory_space=pltpu.HBM)
+    in_vmem = functools.partial(pltpu.with_memory_space_constraint, memory_space=pltpu.VMEM)
+    held = pl.pallas_call(
         functools.partial(kernel, dims),
         out_shape=(
-            jax.ShapeDtypeStruct(base_weights.shape, jnp.float32),
-            jax.ShapeDtypeStruct(momentum.shape, jnp.float32),
-            jax.ShapeDtypeStruct(inner_weights.shape, jnp.bfloat16),
+            pltpu.VMEM(base_weights.shape, jnp.float32),
+            pltpu.VMEM(momentum.shape, jnp.float32),
+            pltpu.VMEM(inner_weights.shape, jnp.bfloat16),
         ),
-        in_specs=[anywhere] * 3,
+        in_specs=[outside] * 3,
         out_specs=(vmem, vmem, vmem),
         scratch_shapes=[
             pltpu.VMEM((local_rows, columns), jnp.float32),
@@ -353,8 +367,16 @@
             dma((shards_count,)),
             dma((shards_count,)),
         ],
-        compiler_params=pltpu.CompilerParams(collective_id=0, has_side_effects=True),
-    )(base_weights, inner_weights, momentum)
+        compiler_params=pltpu.CompilerParams(collective_id=0, has_side_effects=True, vmem_limit_bytes=36 * 2**20),
+    )(in_hbm(base_weights), in_hbm(inner_weights), in_hbm(momentum))
+    return pl.pallas_call(
+        write_out,
+        out_shape=tuple(jax.ShapeDtypeStruct(part.shape, part.dtype) for part in held),
+        in_specs=[vmem] * len(held),
+        out_specs=tuple(outside for part in held),
+        scratch_shapes=[dma((len(held),))],
+        compiler_params=pltpu.CompilerParams(vmem_limit_bytes=2**20),
+    )(*[in_vmem(part) for part in held])
 
 
 def solution(mesh):

time: 64.6 us -> 57.5 us (0.89)
  local copies, waits for them, and re-layouts: 7.24 us -> 0 us
    unnamed x7 -> x0, local copies, waits for them, and re-layouts: 7.24 us -> none
    pallas_call x1 -> x2, Pallas kernels: 56.6 us -> 56.7 us  [the longest x1 53.6 us: shards(): pl.pallas_call(functools.partial(kernel, dims), out_shape=(pltpu.VMEM(bas...]
where the time goes in v2:
time: 57.5 us; the launch traced here: 57.3 us
  Pallas kernels  56.7 us (99%)
  between operations  0.64 us (1%)
    pallas_call x1, Pallas kernels, shards(): pl.pallas_call(functools.partial(kernel, dims), out_shape=(pltpu.VMEM(bas...  53.6 us
    pallas_call x1, Pallas kernels, shards(): pl.pallas_call(write_out, out_shape=tuple((jax.ShapeDtypeStruct(part.shap...  3.04 us

profile of v2, /device:TPU:0, one launch (start us, length us, event | category | flops | bytes accessed | tf_op | source)
XLA Modules:
  0.0 57.3 jit_solution(11163538834453525734)
XLA Ops:
  0.6 53.6 %shard_map.58 = (f32[1024,1024]{1,0:T(8,128)S(1)}, f32[256,1024]{1,0:T(8,128)S(1)}, bf16[1,1024,1024]{2,1,0:T(8,128)(2,1)S(1)}) custom-call(f32[1024,1024]{1,0:T(8,128)} %base_hbm.1, bf16[1,1024,1024]{2,1,0:T(8,128)(2,1)} %inner_hbm.1, f32[256,1024]{1,0:T(8,128)} %momentum_hbm.1), custom_call_target="tpu_custom_call" | custom-call | tf_op jit(solution)/shard_map/pallas_call | solution.py:336
  54.3 3.0 %shard_map.59 = (f32[1024,1024]{1,0:T(8,128)}, f32[256,1024]{1,0:T(8,128)}, bf16[1,1024,1024]{2,1,0:T(8,128)(2,1)}) custom-call(f32[1024,1024]{1,0:T(8,128)S(1)} %get-tuple-element.6.refs_0_, f32[256,1024]{1,0:T(8,128)S(1)} %get-tuple-element.7.refs_1_, bf16[1,1024,1024]{2,1,0:T(8,128)(2,1)S(1)} %get-tuple-element.8.refs_2_), custom_call_target="tpu_custom_call" | custom-call | tf_op jit(solution)/shard_map/pallas_call | solution.py:372

commit v3 on v2

--- a/solution.py
+++ b/solution.py
@@ -8,7 +8,10 @@
 from jax.sharding import PartitionSpec as P
 
 BLOCK = 128
-HALF_GROUPS = 2
+HALF_GROUPS = 4
+EARLY_GROUPS = 2
+ENCODE_ROWS = 256
+PLAIN_ROWS = 64
 
 code_limit = 448.0
 outer_rate = 0.7
@@ -45,7 +48,7 @@
     dims,
     base_hbm, inner_hbm, momentum_hbm,
     new_base, new_momentum, new_inner,
-    base_v, inner_v, momentum_v, dec, first, second, grad, update,
+    base_v, inner_v, momentum_v, dec, first, second, grad, update, early,
     square_mine, square_near, square_row, square_far,
     load_sems, send_one, recv_one, send_two, recv_two, send_all, recv_all,
     near_send, near_recv, far_send, far_recv,
@@ -53,7 +56,8 @@
     replicas, shards_count, rows, columns, groups, total = dims
     width = columns // groups
     span_x, span_y = grid_sides(replicas)
-    tile = min(32, rows)
+    tile = min(PLAIN_ROWS, rows)
+    encode_tile = min(ENCODE_ROWS, rows)
     me = lax.axis_index("replica")
     row_me = lax.axis_index("fsdp")
     me_x, me_y = lax.rem(me, span_x), me // span_x
@@ -98,10 +102,10 @@
         slot = dp * spans(g)[1] + dq
         start = row_start(owner(g, dp, dq))
 
-        @pl.loop(0, rows // tile)
+        @pl.loop(0, rows // encode_tile)
         def _(t):
-            at = pl.ds(pl.multiple_of(start + t * tile, tile), tile)
-            to = pl.ds(pl.multiple_of(t * tile, tile), tile)
+            at = pl.ds(pl.multiple_of(start + t * encode_tile, encode_tile), encode_tile)
+            to = pl.ds(pl.multiple_of(t * encode_tile, encode_tile), encode_tile)
             for c in range(0, width, BLOCK):
                 cols = pl.ds(g * width + c, BLOCK)
                 deltas = base_v[at, cols] - inner_v[at, cols].astype(jnp.float32)
@@ -125,8 +129,9 @@
     def copy_all(g, dp, dq, source):
         np, nq = spans(g)
         slot = ((np - dp) % np) * nq + (source if dp else (nq - dq) % nq)
+        blocks = early if g < EARLY_GROUPS else update
         return pltpu.make_async_remote_copy(
-            src_ref=update.at[g, source if dp else 0], dst_ref=update.at[g, slot],
+            src_ref=blocks.at[g, source if dp else 0], dst_ref=blocks.at[g, slot],
             send_sem=send_all.at[g, slot], recv_sem=recv_all.at[g, slot],
             device_id={"replica": owner(g, dp, dq)}, device_id_type=MESH,
         )
@@ -209,6 +214,7 @@
         squares = lax.fori_loop(0, rows // tile, add, squares)
 
     square_mine[...] = squares
+    square_near[0] = squares
     near_copies = []
     for step in range(1, replicas):
         copy = pltpu.make_async_remote_copy(
@@ -219,11 +225,33 @@
         copy.start()
         near_copies.append(copy)
     sends += near_copies
+
+    momentum_load.wait()
+    for g in range(EARLY_GROUPS):
+        @pl.loop(0, rows // tile)
+        def _(t):
+            at = pl.ds(pl.multiple_of(t * tile, tile), tile)
+            cols = pl.ds(g * width, width)
+            early[g, 0, 0, at] = grad[at, cols].astype(jnp.bfloat16)
+            early[g, 0, 1, at] = momentum_v[at, cols].astype(jnp.bfloat16)
+
+        for dq in range(1, spans(g)[1]):
+            copy = copy_all(g, 0, dq, 0)
+            copy.start()
+            sends.append(copy)
+    for g in range(EARLY_GROUPS):
+        for dp in range(1, spans(g)[0]):
+            copy = copy_all(g, dp, 0, 0)
+            copy.start()
+            sends.append(copy)
+
     for copy in near_copies:
         copy.wait_recv()
-    for step in range(1, replicas):
-        squares += square_near[step]
+    squares = square_near[me]
+    for at in range(1, replicas):
+        squares += square_near[lax.rem(me + replicas - at, replicas)]
     square_row[...] = squares
+    square_far[0] = squares
     far_copies = []
     for step in range(1, shards_count):
         copy = pltpu.make_async_remote_copy(
@@ -234,58 +262,8 @@
         copy.start()
         far_copies.append(copy)
     sends += far_copies
-    momentum_load.wait()
-    for copy in far_copies:
-        copy.wait_recv()
-    for step in range(1, shards_count):
-        squares += square_far[step]
-    mean_square = jnp.full((1, BLOCK), jnp.sum(squares), jnp.float32) / total
-    clip_factor = jnp.minimum(1.0, clip_rms / jnp.sqrt(mean_square + epsilon))
-
-    for g in range(groups):
-        np, nq = spans(g)
-
-        @pl.loop(0, rows // tile)
-        def _(t):
-            at = pl.ds(pl.multiple_of(t * tile, tile), tile)
-            for c in range(0, width, BLOCK):
-                cols = pl.ds(g * width + c, BLOCK)
-                step_term = clip_factor * grad[at, cols]
-                moved = outer_momentum * momentum_v[at, cols] + step_term
-                new_momentum[at, cols] = moved
-                update[g, 0, at, pl.ds(c, BLOCK)] = (step_term + outer_momentum * moved).astype(
-                    jnp.bfloat16
-                )
-
-        for dq in range(1, nq):
-            copy = copy_all(g, 0, dq, 0)
-            copy.start()
-            sends.append(copy)
-    for g in range(groups):
-        for dp in range(1, spans(g)[0]):
-            copy = copy_all(g, dp, 0, 0)
-            copy.start()
-            sends.append(copy)
-
-    def finish(g, dp, dq):
-        slot = dp * spans(g)[1] + dq
-        start = row_start(owner(g, dp, dq))
-
-        @pl.loop(0, rows // tile)
-        def _(t):
-            at = pl.ds(pl.multiple_of(start + t * tile, tile), tile)
-            to = pl.ds(pl.multiple_of(t * tile, tile), tile)
-            cols = pl.ds(g * width, width)
-            fresh = base_v[at, cols] - outer_rate * update[g, slot, to].astype(jnp.float32)
-            new_base[at, cols] = fresh
-            blended = blend_share * inner_v[at, cols].astype(jnp.float32) + (
-                1.0 - blend_share
-            ) * fresh
-            new_inner[0, at, cols] = blended.astype(jnp.bfloat16)
-
-    for g in range(groups):
-        finish(g, 0, 0)
-    for g in range(groups):
+
+    def pass_on(g):
         np, nq = spans(g)
         for dq in range(1, nq):
             copy_all(g, 0, (nq - dq) % nq, 0).wait_recv()
@@ -293,14 +271,91 @@
                 copy = copy_all(g, dp, 0, dq)
                 copy.start()
                 sends.append(copy)
+
+    for g in range(EARLY_GROUPS):
+        pass_on(g)
+    for copy in far_copies:
+        copy.wait_recv()
+    squares = square_far[row_me]
+    for at in range(1, shards_count):
+        squares += square_far[lax.rem(row_me + shards_count - at, shards_count)]
+    mean_square = jnp.full((1, BLOCK), jnp.sum(squares), jnp.float32) / total
+    clip_factor = jnp.minimum(1.0, clip_rms / jnp.sqrt(mean_square + epsilon))
+
+    def moved_and_change(outer, kept):
+        step_term = clip_factor * outer
+        moved = outer_momentum * kept + step_term
+        return moved, step_term + outer_momentum * moved
+
+    def advance(g):
+        @pl.loop(0, rows // tile)
+        def _(t):
+            at = pl.ds(pl.multiple_of(t * tile, tile), tile)
+            for c in range(0, width, BLOCK):
+                cols = pl.ds(g * width + c, BLOCK)
+                moved, change = moved_and_change(grad[at, cols], momentum_v[at, cols])
+                new_momentum[at, cols] = moved
+                if g >= EARLY_GROUPS:
+                    update[g, 0, at, pl.ds(c, BLOCK)] = change.astype(jnp.bfloat16)
+
+    for g in range(EARLY_GROUPS, groups):
+        advance(g)
+        for dq in range(1, spans(g)[1]):
+            copy = copy_all(g, 0, dq, 0)
+            copy.start()
+            sends.append(copy)
+    for g in range(EARLY_GROUPS, groups):
+        for dp in range(1, spans(g)[0]):
+            copy = copy_all(g, dp, 0, 0)
+            copy.start()
+            sends.append(copy)
+
+    def finish(g, dp, dq):
+        slot = dp * spans(g)[1] + dq
+        start = row_start(owner(g, dp, dq))
+
+        @pl.loop(0, rows // tile)
+        def _(t):
+            at = pl.ds(pl.multiple_of(start + t * tile, tile), tile)
+            to = pl.ds(pl.multiple_of(t * tile, tile), tile)
+            for c in range(0, width, BLOCK):
+                cols = pl.ds(g * width + c, BLOCK)
+                from_cols = pl.ds(c, BLOCK)
+                if g < EARLY_GROUPS:
+                    _, change = moved_and_change(
+                        early[g, slot, 0, to, from_cols].astype(jnp.float32),
+                        early[g, slot, 1, to, from_cols].astype(jnp.float32),
+                    )
+                else:
+                    change = update[g, slot, to, from_cols].astype(jnp.float32)
+                fresh = base_v[at, cols] - outer_rate * change
+                new_base[at, cols] = fresh
+                blended = blend_share * inner_v[at, cols].astype(jnp.float32) + (
+                    1.0 - blend_share
+                ) * fresh
+                new_inner[0, at, cols] = blended.astype(jnp.bfloat16)
+
+    def finish_last(g, dq):
+        np = spans(g)[0]
+        for dp in range(1, np):
+            copy_all(g, (np - dp) % np, 0, dq).wait_recv()
+            finish(g, dp, dq)
+
+    for g in range(EARLY_GROUPS):
+        advance(g)
+        for dq in range(spans(g)[1]):
+            finish(g, 0, dq)
+    for g in range(EARLY_GROUPS, groups):
+        finish(g, 0, 0)
+    for g in range(EARLY_GROUPS, groups):
+        pass_on(g)
+    for g in range(EARLY_GROUPS, groups):
+        for dq in range(1, spans(g)[1]):
             finish(g, 0, dq)
     for dq in range(most):
         for g in range(groups):
-            np, nq = spans(g)
-            if dq < nq:
-                for dp in range(1, np):
-                    copy_all(g, (np - dp) % np, 0, dq).wait_recv()
-                    finish(g, dp, dq)
+            if dq < spans(g)[1]:
+                finish_last(g, dq)
     for copy in sends:
         copy.wait_send()
 
@@ -351,6 +406,7 @@
             pltpu.VMEM((groups, most, rows, width), jnp.bfloat16),
             pltpu.VMEM((rows, columns), jnp.float32),
             pltpu.VMEM(blocks, jnp.bfloat16),
+            pltpu.VMEM((max(EARLY_GROUPS, 1), replicas, 2, rows, width), jnp.bfloat16),
             pltpu.VMEM((8, BLOCK), jnp.float32),
             pltpu.VMEM((replicas, 8, BLOCK), jnp.float32),
             pltpu.VMEM((8, BLOCK), jnp.float32),

time: 57.5 us -> 53.8 us (0.936)
  Pallas kernels: 56.7 us -> 53 us
    pallas_call x1, Pallas kernels: 53.6 us -> 49.9 us  [shards(): pl.pallas_call(functools.partial(kernel, dims), out_shape=(pltpu.VMEM(bas...]
where the time goes in v3:
time: 53.8 us; the launch traced here: 53.6 us
  Pallas kernels  53 us (99%)
  between operations  0.64 us (1%)
    pallas_call x1, Pallas kernels, shards(): pl.pallas_call(functools.partial(kernel, dims), out_shape=(pltpu.VMEM(bas...  49.9 us
    pallas_call x1, Pallas kernels, shards(): pl.pallas_call(write_out, out_shape=tuple((jax.ShapeDtypeStruct(part.shap...  3.04 us

profile of v3, /device:TPU:0, one launch (start us, length us, event | category | flops | bytes accessed | tf_op | source)
XLA Modules:
  0.0 53.6 jit_solution(7740622481859818745)
XLA Ops:
  0.6 49.9 %shard_map.58 = (f32[1024,1024]{1,0:T(8,128)S(1)}, f32[256,1024]{1,0:T(8,128)S(1)}, bf16[1,1024,1024]{2,1,0:T(8,128)(2,1)S(1)}) custom-call(f32[1024,1024]{1,0:T(8,128)} %base_hbm.1, bf16[1,1024,1024]{2,1,0:T(8,128)(2,1)} %inner_hbm.1, f32[256,1024]{1,0:T(8,128)} %momentum_hbm.1), custom_call_target="tpu_custom_call" | custom-call | tf_op jit(solution)/shard_map/pallas_call | solution.py:391
  50.6 3.0 %shard_map.59 = (f32[1024,1024]{1,0:T(8,128)}, f32[256,1024]{1,0:T(8,128)}, bf16[1,1024,1024]{2,1,0:T(8,128)(2,1)}) custom-call(f32[1024,1024]{1,0:T(8,128)S(1)} %get-tuple-element.6.refs_0_, f32[256,1024]{1,0:T(8,128)S(1)} %get-tuple-element.7.refs_1_, bf16[1,1024,1024]{2,1,0:T(8,128)(2,1)S(1)} %get-tuple-element.8.refs_2_), custom_call_target="tpu_custom_call" | custom-call | tf_op jit(solution)/shard_map/pallas_call | solution.py:428

commit v4 on v3

--- a/solution.py
+++ b/solution.py
@@ -11,7 +11,7 @@
 HALF_GROUPS = 4
 EARLY_GROUPS = 2
 ENCODE_ROWS = 256
-PLAIN_ROWS = 64
+PLAIN_ROWS = 128
 
 code_limit = 448.0
 outer_rate = 0.7
@@ -78,6 +78,12 @@
     def row_start(index):
         return pl.multiple_of(index * rows, rows)
 
+    barrier = pltpu.get_barrier_semaphore()
+    for step in range(1, replicas):
+        pl.semaphore_signal(barrier, inc=1, device_id={"replica": near(step)}, device_id_type=MESH)
+    for step in range(1, shards_count):
+        pl.semaphore_signal(barrier, inc=1, device_id={"fsdp": far(step)}, device_id_type=MESH)
+
     load_order = [(dx, dy) for dy in reversed(range(span_y)) for dx in reversed(range(span_x))]
     loads = []
     for at, (dx, dy) in enumerate(load_order):
@@ -91,12 +97,6 @@
         loads.append(pair)
     momentum_load = pltpu.make_async_copy(momentum_hbm, momentum_v, load_sems.at[replicas, 0])
     momentum_load.start()
-
-    barrier = pltpu.get_barrier_semaphore()
-    for step in range(1, replicas):
-        pl.semaphore_signal(barrier, inc=1, device_id={"replica": near(step)}, device_id_type=MESH)
-    for step in range(1, shards_count):
-        pl.semaphore_signal(barrier, inc=1, device_id={"fsdp": far(step)}, device_id_type=MESH)
 
     def encode(g, dp, dq):
         slot = dp * spans(g)[1] + dq

time: 53.8 us -> 53.7 us (level)
  no operation moved by 1% of the time
where the time goes in v4:
time: 53.7 us; the launch traced here: 53.5 us
  Pallas kernels  52.9 us (99%)
  between operations  0.64 us (1%)
    pallas_call x1, Pallas kernels, shards(): pl.pallas_call(functools.partial(kernel, dims), out_shape=(pltpu.VMEM(bas...  49.8 us
    pallas_call x1, Pallas kernels, shards(): pl.pallas_call(write_out, out_shape=tuple((jax.ShapeDtypeStruct(part.shap...  3.04 us

profile of v4, /device:TPU:0, one launch (start us, length us, event | category | flops | bytes accessed | tf_op | source)
XLA Modules:
  0.0 53.5 jit_solution(8661009172716560218)
XLA Ops:
  0.6 49.8 %shard_map.58 = (f32[1024,1024]{1,0:T(8,128)S(1)}, f32[256,1024]{1,0:T(8,128)S(1)}, bf16[1,1024,1024]{2,1,0:T(8,128)(2,1)S(1)}) custom-call(f32[1024,1024]{1,0:T(8,128)} %base_hbm.1, bf16[1,1024,1024]{2,1,0:T(8,128)(2,1)} %inner_hbm.1, f32[256,1024]{1,0:T(8,128)} %momentum_hbm.1), custom_call_target="tpu_custom_call" | custom-call | tf_op jit(solution)/shard_map/pallas_call | solution.py:391
  50.5 3.0 %shard_map.59 = (f32[1024,1024]{1,0:T(8,128)}, f32[256,1024]{1,0:T(8,128)}, bf16[1,1024,1024]{2,1,0:T(8,128)(2,1)}) custom-call(f32[1024,1024]{1,0:T(8,128)S(1)} %get-tuple-element.6.refs_0_, f32[256,1024]{1,0:T(8,128)S(1)} %get-tuple-element.7.refs_1_, bf16[1,1024,1024]{2,1,0:T(8,128)(2,1)S(1)} %get-tuple-element.8.refs_2_), custom_call_target="tpu_custom_call" | custom-call | tf_op jit(solution)/shard_map/pallas_call | solution.py:428
